TPU v7x, 8 devices: a whole 2x2x1 slice. The times are simulated.
8 devices in a mesh: dp: 1 (over z), ep: 8 (over y, x, core).
Axes of the slice: x: 2, y: 2, z: 1, core: 2. Of those that a mesh axis runs over, the one named last changes fastest.
Arguments:
- hidden_in: bfloat16 [2048, 2560], P(('dp', 'ep'))
- norm_gain: float32 [2560], replicated
- router_w: float32 [64, 2560], replicated
- w_gate: bfloat16 [64, 2560, 1536], P('ep')
- w_up: bfloat16 [64, 2560, 1536], P('ep')
- w_down: bfloat16 [64, 1536, 2560], P('ep')
- ws_gate: bfloat16 [2560, 3072], replicated
- ws_up: bfloat16 [2560, 3072], replicated
- ws_down: bfloat16 [3072, 2560], replicated
- expert_ids: int32 [2048, 6], P(('dp', 'ep'))
Outputs:
- output: bfloat16 [2048, 2560], P(('dp', 'ep'))
All inputs are finite; a program needn't handle non-finite values.
Results may differ from a plain program's by a relative error of at most 0.00440109.
Values are sent between devices in bfloat16 or wider.
A program may use at most 1 GiB of HBM per device.

v0:
```python
import jax
import jax.numpy as jnp
from jax import lax
from jax.sharding import PartitionSpec as P

NORM_EPS = 1e-6
ROUTE_SCALE = 2.5
GROUPS = 8
GROUP_LIMIT = 4


def rms_norm(x_rows, norm_gain):
    x_f32 = x_rows.astype(jnp.float32)
    inv_rms = lax.rsqrt(jnp.mean(x_f32 * x_f32, axis=-1, keepdims=True) + NORM_EPS)
    return (x_f32 * inv_rms * norm_gain).astype(jnp.bfloat16)


def route_gates(x_norm, router_w, expert_ids):
    logits = jnp.einsum("td,nd->tn", x_norm.astype(jnp.float32), router_w, precision=lax.Precision.HIGHEST, preferred_element_type=jnp.float32)
    picked = jnp.take_along_axis(jax.nn.sigmoid(logits), expert_ids, axis=1)
    return ROUTE_SCALE * picked / jnp.sum(picked, axis=1, keepdims=True)


def swiglu(tok_rows, gate_mat, up_mat, down_mat):
    h_gate = jnp.dot(tok_rows, gate_mat, preferred_element_type=jnp.float32)
    h_up = jnp.dot(tok_rows, up_mat, preferred_element_type=jnp.float32)
    hidden = (jax.nn.silu(h_gate) * h_up).astype(jnp.bfloat16)
    return jnp.dot(hidden, down_mat, preferred_element_type=jnp.float32).astype(jnp.bfloat16)


def expert_stack(expert_in, w_gate, w_up, w_down):
    h_gate = jnp.einsum("ecd,edi->eci", expert_in, w_gate, preferred_element_type=jnp.float32)
    h_up = jnp.einsum("ecd,edi->eci", expert_in, w_up, preferred_element_type=jnp.float32)
    hidden = (jax.nn.silu(h_gate) * h_up).astype(jnp.bfloat16)
    return jnp.einsum("eci,eid->ecd", hidden, w_down, preferred_element_type=jnp.float32).astype(jnp.bfloat16)


def solution(mesh):
    ep_size = mesh.shape["ep"]

    def local_block(hidden_in, norm_gain, router_w, w_gate, w_up, w_down, ws_gate, ws_up, ws_down, expert_ids):
        tok_dev, top_k = expert_ids.shape
        model_dim = hidden_in.shape[1]
        exp_dev = w_gate.shape[0]
        pair_cap = GROUPS * ((top_k + GROUP_LIMIT - 1) // GROUP_LIMIT) * tok_dev // ep_size
        recv_cap = pair_cap * ep_size
        exp_cap = recv_cap // exp_dev
        x_norm = rms_norm(hidden_in, norm_gain)
        gate_vals = route_gates(x_norm, router_w, expert_ids)
        shared_out = swiglu(x_norm, ws_gate, ws_up, ws_down)

        flat_ids = expert_ids.reshape(-1)
        dest_dev = flat_ids // exp_dev
        dest_hot = (dest_dev[:, None] == jnp.arange(ep_size, dtype=jnp.int32)[None, :]).astype(jnp.int32)
        dest_rank = jnp.sum((jnp.cumsum(dest_hot, axis=0) - 1) * dest_hot, axis=1)
        send_slot = dest_dev * pair_cap + dest_rank
        pair_tok = jnp.arange(tok_dev * top_k, dtype=jnp.int32) // top_k
        slot_tok = jnp.full((recv_cap,), tok_dev, jnp.int32).at[send_slot].set(pair_tok)
        slot_exp = jnp.full((recv_cap,), -1, jnp.int32).at[send_slot].set(flat_ids % exp_dev)
        send_rows = jnp.take(x_norm, slot_tok, axis=0, mode="fill", fill_value=0)
        recv_rows = lax.all_to_all(send_rows, "ep", 0, 0, tiled=True)
        recv_exp = lax.all_to_all(slot_exp, "ep", 0, 0, tiled=True)

        exp_hot = (recv_exp[:, None] == jnp.arange(exp_dev, dtype=jnp.int32)[None, :]).astype(jnp.int32)
        exp_rank = jnp.sum((jnp.cumsum(exp_hot, axis=0) - 1) * exp_hot, axis=1)
        buf_slot = jnp.where(recv_exp >= 0, recv_exp * exp_cap + exp_rank, recv_cap)
        buf_row = jnp.full((recv_cap,), recv_cap, jnp.int32).at[buf_slot].set(jnp.arange(recv_cap, dtype=jnp.int32), mode="drop")
        expert_in = jnp.take(recv_rows, buf_row, axis=0, mode="fill", fill_value=0).reshape(exp_dev, exp_cap, model_dim)
        expert_out = expert_stack(expert_in, w_gate, w_up, w_down).reshape(recv_cap, model_dim)
        back_rows = jnp.take(expert_out, buf_slot, axis=0, mode="fill", fill_value=0)
        returned = lax.all_to_all(back_rows, "ep", 0, 0, tiled=True)

        pair_out = jnp.take(returned, send_slot, axis=0).reshape(tok_dev, top_k, model_dim)
        routed = jnp.sum(gate_vals[:, :, None] * pair_out.astype(jnp.float32), axis=1)
        return (hidden_in.astype(jnp.float32) + shared_out.astype(jnp.float32) + routed).astype(jnp.bfloat16)

    row_spec = P(("dp", "ep"), None)
    in_specs = (row_spec, P(), P(), P("ep"), P("ep"), P("ep"), P(), P(), P(), row_spec)
    return jax.shard_map(local_block, mesh=mesh, in_specs=in_specs, out_specs=row_spec, check_vma=False)
```

profile of v0, /device:TPU:0, one launch (start us, length us, event | category | flops | bytes accessed | tf_op | source)
XLA Modules:
  0.0 895.1 jit_solution(2380880199065749853)
XLA Ops:
  0.0 0.9 copy.36
  1.4 2.3 reduce-window.14
  4.9 6.7 scatter_custom_fusion.1
  11.7 4.3 all-to-all-start.1
  16.0 6.2 scatter_custom_fusion
  22.2 1.7 fusion.4
  23.9 1.7 fusion.6
  25.6 22.1 %gather_fusion = bf16[4096,2560]{1,0:T(8,128)(2,1)} fusion(bf16[256,2560]{1,0:T(8,128)(2,1)S(1)} %fusion.6, s32[4096]{0:T(1024)S(1)} %fusion.16), kind=kCustom, calls=%fused_computation.2 | custom fusion | bytes 41959424 | tf_op jit(solution)/shard_map/jit(_take)/gather | solution.py:60
  47.8 17.5 %broadcast_select_fusion.2 = bf16[8,512,2560]{2,1,0:T(8,128)(2,1)} fusion(bf16[8,512,2560]{2,1,0:T(8,128)(2,1)} %bitcast.70, pred[8,512]{1,0:T(8,128)(4,1)S(1)} %broadcast_in_dim.59), kind=kLoop, calls=%fused_computation.12 | loop fusion | flops 10485760 | bytes 41947136 | tf_op jit(solution)/shard_map/jit(_take)/select_n | solution.py:60
  65.3 4.8 all-to-all-start
  70.1 2.3 reduce-window.16
  73.3 15.5 %scatter_custom_fusion.2 = s32[4096]{0:T(1024)S(1)} fusion(s32[4096]{0:T(1024)S(1)} %bitcast.82, s32[4096]{0:T(1024)S(1)} %iota.21, s32[]{:T(128)} %constant.119.clone.1), kind=kCustom, calls=%fused_computation.92 | custom fusion | bytes 16388 | tf_op jit(solution)/shard_map/scatter | solution.py:67
  88.9 0.6 compare_and_fusion
  89.5 0.6 broadcast_clamp_fusion
  90.1 209.0 %all-to-all-done = bf16[8,512,2560]{2,1,0:T(8,128)(2,1)} async-done(((bf16[8,512,2560]{2,1,0:T(8,128)(2,1)}), bf16[8,512,2560]{2,1,0:T(8,128)(2,1)}, u32[]{:S(2)}, u32[]{:S(2)}) %all-to-all-start) | async-done | bytes 20971552 | tf_op jit(solution)/shard_map/all_to_all | solution.py:61
  299.1 47.5 %gather_fusion.3 = bf16[4096,2560]{1,0:T(8,128)(2,1)} fusion(bf16[4096,2560]{1,0:T(8,128)(2,1)} %bitcast.11, s32[4096]{0:T(1024)S(1)} %fusion.17), kind=kCustom, calls=%fused_computation.clone | custom fusion | bytes 41959424 | tf_op jit(solution)/shard_map/jit(_take)/gather | solution.py:68
  346.5 18.5 %broadcast_select_fusion.1 = bf16[4096,2560]{1,0:T(8,128)(2,1)} fusion(bf16[4096,2560]{1,0:T(8,128)(2,1)} %gather_fusion.3, pred[4096]{0:T(1024)(128)(4,1)S(1)} %compare_and_fusion.1), kind=kLoop, calls=%fused_computation.11 | loop fusion | flops 10485760 | bytes 41947136 | tf_op jit(solution)/shard_map/jit(_take)/select_n | solution.py:68
  365.0 47.0 %fusion.39 = f32[8,512,1536]{2,1,0:T(8,128)} fusion(bf16[8,512,2560]{2,1,0:T(8,128)(2,1)} %bitcast.71, bf16[8,2560,1536]{2,1,0:T(8,128)(2,1)} %param.15), kind=kOutput, calls=%fused_computation.112 | convolution fusion | flops 32212254720 | bytes 109051904 | tf_op jit(solution)/shard_map/ecd,edi->eci/dot_general | solution.py:32
  412.1 56.1 %multiply_convert_fusion.clone.4 = bf16[8,512,1536]{2,1,0:T(8,128)(2,1)} fusion(f32[8,512,1536]{2,1,0:T(8,128)} %fusion.39, bf16[8,512,2560]{2,1,0:T(8,128)(2,1)} %bitcast.72, bf16[8,2560,1536]{2,1,0:T(8,128)(2,1)} %param.16), kind=kOutput, calls=%fused_computation.8.clone.clone.clone.1 | convolution fusion | flops 32250003456 | bytes 121634816 | tf_op jit(solution)/shard_map/ecd,edi->eci/dot_general | solution.py:33
  468.2 48.4 %convolution_convert_fusion = bf16[8,512,2560]{2,1,0:T(8,128)(2,1)} fusion(bf16[8,1536,2560]{2,1,0:T(8,128)(2,1)} %param.17, bf16[8,512,1536]{2,1,0:T(8,128)(2,1)} %multiply_convert_fusion.clone.4), kind=kOutput, calls=%fused_computation.13 | convolution fusion | flops 32222740480 | bytes 96468992 | tf_op jit(solution)/shard_map/eci,eid->ecd/dot_general | solution.py:35
  516.6 47.3 %gather_fusion.4 = bf16[4096,2560]{1,0:T(8,128)(2,1)} fusion(bf16[4096,2560]{1,0:T(8,128)(2,1)} %bitcast.68, s32[4096]{0:T(1024)S(1)} %copy-done.7), kind=kCustom, calls=%fused_computation.1.clone | custom fusion | bytes 41959424 | tf_op jit(solution)/shard_map/jit(_take)/gather | solution.py:70
  563.9 18.5 %broadcast_select_fusion = bf16[4096,2560]{1,0:T(8,128)(2,1)} fusion(bf16[4096,2560]{1,0:T(8,128)(2,1)} %gather_fusion.4, pred[4096]{0:T(1024)(128)(4,1)S(1)} %copy-done.10), kind=kLoop, calls=%fused_computation.10 | loop fusion | flops 10485760 | bytes 41947136 | tf_op jit(solution)/shard_map/jit(_take)/select_n | solution.py:70
  582.4 5.2 all-to-all-start.2
  588.4 1.3 fusion.9
  589.7 12.7 %gather_fusion.2 = f32[1536]{0:T(1024)S(1)} fusion(f32[256,64]{0,1:T(8,128)S(1)} %fusion.9, s32[1536]{0:T(1024)S(1)} %reshape.301), kind=kCustom, calls=%fused_computation.4 | custom fusion | bytes 24576 | tf_op jit(solution)/shard_map/jit(take_along_axis)/gather | solution.py:20
  602.9 7.7 fusion.38
  610.6 11.3 %fusion.2 = bf16[256,3072]{1,0:T(8,128)(2,1)} fusion(bf16[256,2560]{1,0:T(8,128)(2,1)S(1)} %copy-done.2, bf16[2560,3072]{1,0:T(8,128)(2,1)} %param.19, f32[256,3072]{1,0:T(8,128)S(1)} %fusion.38), kind=kOutput, calls=%fused_computation.21 | convolution fusion | flops 4031250432 | bytes 21757952 | tf_op jit(solution)/shard_map/dot_general | solution.py:26
  621.8 194.7 %all-to-all-done.2 = bf16[8,512,2560]{2,1,0:T(8,128)(2,1)} async-done(((bf16[8,512,2560]{2,1,0:T(8,128)(2,1)}), bf16[8,512,2560]{2,1,0:T(8,128)(2,1)}, u32[]{:S(2)}, u32[]{:S(2)}) %all-to-all-start.2) | async-done | bytes 20971552 | tf_op jit(solution)/shard_map/all_to_all | solution.py:71
  816.5 24.8 %gather_fusion.1 = bf16[1536,2560]{1,0:T(8,128)(2,1)} fusion(bf16[4096,2560]{1,0:T(8,128)(2,1)} %bitcast.15, s32[2048]{0:T(1024)S(1)} %pad_clamp_fusion), kind=kCustom, calls=%fused_computation.3 | custom fusion | bytes 15734784 | tf_op jit(solution)/shard_map/jit(_take)/gather | solution.py:73
  841.3 13.1 %gather.23 = bf16[256,6,2560]{2,1,0:T(8,128)(2,1)} reshape(bf16[1536,2560]{1,0:T(8,128)(2,1)} %gather_fusion.1) | data formatting | bytes 15728640 | tf_op jit(solution)/shard_map/jit(_take)/gather | solution.py:73
  854.4 29.0 %multiply_reduce_fusion = f32[256,2560]{1,0:T(8,128)S(1)} fusion(bf16[256,6,2560]{2,1,0:T(8,128)(2,1)} %gather.23, f32[256,6]{1,0:T(8,128)S(1)} %copy.35, pred[256,6]{1,0:T(8,128)(4,1)S(1)} %copy.39), kind=kLoop, calls=%fused_computation.9 | loop fusion | flops 15073280 | bytes 10493440 | tf_op jit(solution)/shard_map/reduce_sum | solution.py:74
  883.4 11.2 %fusion.3 = bf16[256,2560]{1,0:T(8,128)(2,1)} fusion(f32[256,2560]{1,0:T(8,128)S(1)} %multiply_reduce_fusion, bf16[256,3072]{1,0:T(8,128)(2,1)} %fusion.2, bf16[3072,2560]{1,0:T(8,128)(2,1)} %param.20, bf16[256,2560]{1,0:T(8,128)(2,1)S(1)} %copy-done.3), kind=kOutput, calls=%fused_computation.22 | convolution fusion | flops 4030464000 | bytes 22544384 | tf_op jit(solution)/shard_map/dot_general | solution.py:28
  (63 shorter events, 3.7 us)
Async XLA Ops:
  0.0 588.3 %copy-start = (f32[64,2560]{1,0:T(8,128)S(1)}, f32[64,2560]{1,0:T(8,128)}, u32[]{:S(2)}) copy-start(f32[64,2560]{1,0:T(8,128)} %param.14) | copy-start | bytes 1966084
  4.3 0.6 copy-start.5
  4.9 19.0 %copy-start.8 = (s32[1536]{0:T(1024)}, s32[1536]{0:T(1024)S(1)}, u32[]{:S(2)}) copy-start(s32[1536]{0:T(1024)S(1)} %fusion.34) | copy-start | bytes 18436
  11.7 53.6 %all-to-all-start.1 = ((s32[8,512,1]{1,2,0:T(1,128)}), s32[8,512,1]{1,2,0:T(1,128)S(1)}, u32[]{:S(2)}, u32[]{:S(2)}) async-start(s32[8,512,1]{1,2,0:T(1,128)} %bitcast.2), calls=%async_computation.1 | async-start | bytes 32768 | tf_op jit(solution)/shard_map/all_to_all | solution.py:62
  25.6 22.1 %copy-start.1 = (bf16[256,2560]{1,0:T(8,128)(2,1)}, bf16[256,2560]{1,0:T(8,128)(2,1)S(1)}, u32[]{:S(2)}) copy-start(bf16[256,2560]{1,0:T(8,128)(2,1)S(1)} %fusion.6) | copy-start | bytes 3932164
  65.3 233.8 %all-to-all-start = ((bf16[8,512,2560]{2,1,0:T(8,128)(2,1)}), bf16[8,512,2560]{2,1,0:T(8,128)(2,1)}, u32[]{:S(2)}, u32[]{:S(2)}) async-start(bf16[8,512,2560]{2,1,0:T(8,128)(2,1)} %broadcast_select_fusion.2), calls=%async_computation | async-start | bytes 41943040 | tf_op jit(solution)/shard_map/all_to_all | solution.py:61
  468.2 48.4 %copy-start.7 = (s32[4096]{0:T(1024)S(1)}, s32[4096]{0:T(1024)}, u32[]{:S(2)}) copy-start(s32[4096]{0:T(1024)} %broadcast_clamp_fusion) | copy-start | bytes 49156
  516.6 47.3 %copy-start.10 = (pred[4096]{0:T(1024)(128)(4,1)S(1)}, pred[4096]{0:T(1024)(128)(4,1)}, u32[]{:S(2)}) copy-start(pred[4096]{0:T(1024)(128)(4,1)} %compare_and_fusion) | copy-start | bytes 12292
  582.4 5.2 copy-start.6
  582.4 5.4 copy-start.4
  582.4 6.0 copy-start.2
  582.4 234.1 %all-to-all-start.2 = ((bf16[8,512,2560]{2,1,0:T(8,128)(2,1)}), bf16[8,512,2560]{2,1,0:T(8,128)(2,1)}, u32[]{:S(2)}, u32[]{:S(2)}) async-start(bf16[8,512,2560]{2,1,0:T(8,128)(2,1)} %bitcast.69), calls=%async_computation.2 | async-start | bytes 41943040 | tf_op jit(solution)/shard_map/all_to_all | solution.py:71
  589.7 13.2 %copy-start.9 = (s32[1536]{0:T(1024)S(1)}, s32[1536]{0:T(1024)}, u32[]{:S(2)}) copy-start(s32[1536]{0:T(1024)} %copy-done.8) | copy-start | bytes 18436
  841.3 42.1 %copy-start.3 = (bf16[256,2560]{1,0:T(8,128)(2,1)S(1)}, bf16[256,2560]{1,0:T(8,128)(2,1)}, u32[]{:S(2)}) copy-start(bf16[256,2560]{1,0:T(8,128)(2,1)} %param.12) | copy-start | bytes 3932164
where the time goes:
time: 907 us; the launch traced here: 895 us
  waiting for transfers between devices  404 us (45%)
  local copies, waits for them, and re-layouts  200 us (22%)
  matrix products  183 us (20%)
  other arithmetic  93.7 us (10%)
  starting transfers between devices  14.3 us (2%)
    all_to_all x1, waiting for transfers between devices, local_block(): recv_rows = lax.all_to_all(send_rows, 'ep', 0, 0, tiled=True)  209 us
    all_to_all x1, waiting for transfers between devices, local_block(): returned = lax.all_to_all(back_rows, 'ep', 0, 0, tiled=True)  195 us
    dot_general x1, matrix products, expert_stack(): jnp.einsum('ecd,edi->eci', expert_in, w_up, preferred_element_type=jnp.fl...  56.1 us
    dot_general x1, matrix products, expert_stack(): jnp.einsum('eci,eid->ecd', hidden, w_down, preferred_element_type=jnp.flo...  48.4 us
    gather x1, local copies, waits for them, and re-layouts, local_block(): jnp.take(recv_rows, buf_row, axis=0, mode='fill', fill_value=0)  47.5 us
    gather x1, local copies, waits for them, and re-layouts, local_block(): jnp.take(expert_out, buf_slot, axis=0, mode='fill', fill_value=0)  47.3 us
    dot_general x1, matrix products, expert_stack(): jnp.einsum('ecd,edi->eci', expert_in, w_gate, preferred_element_type=jnp....  47 us
    gather x2, local copies, waits for them, and re-layouts, local_block(): jnp.take(returned, send_slot, axis=0).reshape(tok_dev, top_k, model_dim)  37.9 us
  transfers between devices with their start and end apart: 3, of which 2 were waited for; matrix products, arithmetic and copies ran while one was open for 12% of the time, Pallas kernels for 0%

commit v1 on v0

v1 whole, which is shorter than its diff:
```python
import functools

import jax
import jax.numpy as jnp
from jax import lax
from jax.experimental import pallas as pl
from jax.experimental.pallas import tpu as pltpu
from jax.sharding import PartitionSpec as P

NORM_EPS = 1e-6
ROUTE_SCALE = 2.5
LANES = 128
MESH = pl.DeviceIdType.MESH
VMEM_LIMIT = 66_000_000


def rms_norm(x_rows, norm_gain):
    x_f32 = x_rows.astype(jnp.float32)
    inv_rms = lax.rsqrt(jnp.mean(x_f32 * x_f32, axis=-1, keepdims=True) + NORM_EPS)
    return (x_f32 * inv_rms * norm_gain).astype(jnp.bfloat16)


def route_gates(x_norm, router_w, expert_ids):
    logits = jnp.einsum("td,nd->tn", x_norm.astype(jnp.float32), router_w, precision=lax.Precision.HIGHEST, preferred_element_type=jnp.float32)
    scores = jax.nn.sigmoid(logits)
    hot = expert_ids[:, :, None] == jnp.arange(router_w.shape[0], dtype=jnp.int32)[None, None, :]
    picked = jnp.sum(jnp.where(hot, scores[:, None, :], 0.0), axis=2)
    return ROUTE_SCALE * picked / jnp.sum(picked, axis=1, keepdims=True)


def swiglu(tok_rows, gate_mat, up_mat, down_mat):
    h_gate = jnp.dot(tok_rows, gate_mat, preferred_element_type=jnp.float32)
    h_up = jnp.dot(tok_rows, up_mat, preferred_element_type=jnp.float32)
    hidden = (jax.nn.silu(h_gate) * h_up).astype(jnp.bfloat16)
    return jnp.dot(hidden, down_mat, preferred_element_type=jnp.float32).astype(jnp.bfloat16)


def gate_up_kernel(tok_ref, xn_ref, wg_ref, wu_ref, h_ref, xf, gbuf, lhs):
    e = pl.program_id(0)
    j = pl.program_id(1)
    cap, d = lhs.shape
    nc = d // LANES

    @pl.when((e == 0) & (j == 0))
    def _():
        def widen(b, _):
            rows = pl.multiple_of(b * 64, 64)
            blk = xn_ref[pl.ds(rows, 64), :].astype(jnp.float32)
            for c in range(nc):
                xf[pl.ds(rows * nc + c, 64, stride=nc), :] = blk[:, c * LANES:(c + 1) * LANES]
            return 0
        lax.fori_loop(0, xn_ref.shape[0] // 64, widen, 0)

    @pl.when(j == 0)
    def _():
        def gather(b, _):
            for u in range(16):
                r = b * 16 + u
                gbuf[pl.ds(r * nc, nc), :] = xf[pl.ds(tok_ref[e * cap + r], nc), :]
            return 0
        lax.fori_loop(0, cap // 16, gather, 0)

        def narrow(b, _):
            rows = pl.multiple_of(b * 64, 64)
            for c in range(nc):
                lhs[pl.ds(rows, 64), c * LANES:(c + 1) * LANES] = gbuf[pl.ds(rows * nc + c, 64, stride=nc), :].astype(jnp.bfloat16)
            return 0
        lax.fori_loop(0, cap // 64, narrow, 0)

    g = jnp.dot(lhs[...], wg_ref[0], preferred_element_type=jnp.float32)
    u = jnp.dot(lhs[...], wu_ref[0], preferred_element_type=jnp.float32)
    h_ref[0] = (g * jax.nn.sigmoid(g) * u).astype(jnp.bfloat16)


def gate_up(tok_off, xn_all, w_gate, w_up, block=512):
    n_exp, d, inter = w_gate.shape
    cap = tok_off.shape[0] // n_exp
    tokens = xn_all.shape[0]
    return pl.pallas_call(
        gate_up_kernel,
        grid_spec=pltpu.PrefetchScalarGridSpec(
            num_scalar_prefetch=1,
            grid=(n_exp, inter // block),
            in_specs=[
                pl.BlockSpec((tokens, d), lambda e, j, t: (0, 0), pipeline_mode=pl.Buffered(1)),
                pl.BlockSpec((1, d, block), lambda e, j, t: (e, 0, j)),
                pl.BlockSpec((1, d, block), lambda e, j, t: (e, 0, j)),
            ],
            out_specs=pl.BlockSpec((1, cap, block), lambda e, j, t: (e, 0, j)),
            scratch_shapes=[
                pltpu.VMEM((tokens * d // LANES, LANES), jnp.float32),
                pltpu.VMEM((cap * d // LANES, LANES), jnp.float32),
                pltpu.VMEM((cap, d), jnp.bfloat16),
            ],
        ),
        out_shape=jax.ShapeDtypeStruct((n_exp, cap, inter), jnp.bfloat16),
        compiler_params=pltpu.CompilerParams(vmem_limit_bytes=VMEM_LIMIT, dimension_semantics=("arbitrary", "arbitrary")),
        cost_estimate=pl.CostEstimate(flops=4 * n_exp * cap * d * inter, bytes_accessed=4 * n_exp * d * inter, transcendentals=0),
        name="gate_up",
    )(tok_off, xn_all, w_gate, w_up)


def neighbours():
    me = lax.axis_index("ep")
    core, bx, by = lax.rem(me, 2), lax.rem(me // 2, 2), me // 4
    return core, bx, by, me + 1 - 2 * core, me + 2 - 4 * bx, me + 4 - 8 * by


def down_kernel(cw, slot_ref, h_hbm, wd_hbm, gate_ref, base_ref, out_ref,
                h, wd, ybuf, part, got_core, got_x, got_y, got_xy, got_yx,
                h_sem, wd_sem, send_core, recv_core, send_x, recv_x, send_y, recv_y, send_2, recv_2):
    n_exp, cap, inter = h.shape
    d = base_ref.shape[1]
    n_chunk, sub = d // cw, cw // LANES
    rows = part.shape[2] // 2
    tok_dev = part.shape[2] // sub
    n_dev = 8
    top = 6
    core, bx, by, partner, xdev, ydev = neighbours()

    barrier = pltpu.get_barrier_semaphore()
    for dev in (partner, xdev, ydev):
        pl.semaphore_signal(barrier, inc=1, device_id={"ep": dev}, device_id_type=MESH)

    def h_copy(e):
        return pltpu.make_async_copy(h_hbm.at[e], h.at[e], h_sem.at[e])

    def wd_copy(s):
        c, e = s // n_exp, lax.rem(s, n_exp)
        slot = lax.rem(s, 3)
        return pltpu.make_async_copy(wd_hbm.at[e, :, pl.ds(pl.multiple_of(c * cw, LANES), cw)], wd.at[slot], wd_sem.at[slot])

    for e in range(n_exp):
        h_copy(e).start()
    n_step = n_chunk * n_exp
    wd_copy(0).start()
    wd_copy(1).start()
    ybuf[pl.ds(n_exp * cap * sub, 8), :] = jnp.zeros((8, LANES), jnp.float32)
    pl.semaphore_wait(barrier, 3)

    def remote(src, dst, send, recv, dev):
        return pltpu.make_async_remote_copy(src_ref=src, dst_ref=dst, send_sem=send, recv_sem=recv, device_id={"ep": dev}, device_id_type=MESH)

    def copy_core(c):
        p = lax.rem(c, 2)
        return [remote(part.at[p, 2 * q + 1 - core], got_core.at[c, q], send_core.at[p, q], recv_core.at[c, q], partner) for q in range(4)]

    def copy_x(c):
        return [remote(got_core.at[c, 2 * yy + 1 - bx, pl.ds(0, rows)], got_x.at[c, yy], send_x.at[c, yy], recv_x.at[c, yy], xdev) for yy in range(2)]

    def copy_y(c):
        return [remote(got_core.at[c, 2 * (1 - by) + xx, pl.ds(rows, rows)], got_y.at[c, xx], send_y.at[c, xx], recv_y.at[c, xx], ydev) for xx in range(2)]

    def copy_2(c):
        return [
            remote(got_core.at[c, 2 * (1 - by) + bx, pl.ds(0, rows)], got_xy.at[c], send_2.at[c, 0], recv_2.at[c, 0], ydev),
            remote(got_core.at[c, 2 * by + 1 - bx, pl.ds(rows, rows)], got_yx.at[c], send_2.at[c, 1], recv_2.at[c, 1], xdev),
        ]

    def add_into(dst, src, n):
        def one(i, _):
            at = pl.ds(pl.multiple_of(i * 64, 64), 64)
            dst[at, :] = dst[at, :] + src[at, :]
            return 0
        lax.fori_loop(0, n // 64, one, 0)

    def on_core(c):
        p = lax.rem(c, 2)
        for q, cp in enumerate(copy_core(c)):
            cp.wait_recv()
            add_into(got_core.at[c, q], part.at[p, 2 * q + core], 2 * rows)
        for cp in copy_x(c) + copy_y(c):
            cp.start()

    def on_first(c):
        for yy, cp in enumerate(copy_x(c)):
            cp.wait_recv()
            add_into(got_core.at[c, 2 * yy + bx, pl.ds(0, rows)], got_x.at[c, yy], rows)
        for xx, cp in enumerate(copy_y(c)):
            cp.wait_recv()
            add_into(got_core.at[c, 2 * by + xx, pl.ds(rows, rows)], got_y.at[c, xx], rows)
        for cp in copy_2(c):
            cp.start()

    def on_second(c):
        a, b = copy_2(c)
        mine = got_core.at[c, 2 * by + bx]
        a.wait_recv()
        add_into(mine.at[pl.ds(0, rows)], got_xy.at[c], rows)
        b.wait_recv()
        add_into(mine.at[pl.ds(rows, rows)], got_yx.at[c], rows)

    def down(c, lo, hi):
        def one(e, _):
            s = c * n_exp + e
            slot = lax.rem(s, 3)
            @pl.when(s + 2 < n_step)
            def _():
                wd_copy(s + 2).start()
            @pl.when(c == 0)
            def _():
                h_copy(e).wait()
            wd_copy(s).wait()
            y = jnp.dot(h[e], wd[slot], preferred_element_type=jnp.float32)
            y = y.astype(jnp.bfloat16).astype(jnp.float32) * gate_ref[e]
            for i in range(sub):
                ybuf[pl.ds(e * (cap * sub) + i, cap, stride=sub), :] = y[:, i * LANES:(i + 1) * LANES]
            return 0
        lax.fori_loop(lo, hi, one, 0)

    def combine(c):
        p = lax.rem(c, 2)
        def dev_loop(dev, _):
            def one(b, _):
                for u in range(8):
                    t = b * 8 + u
                    acc = None
                    for k in range(top):
                        row = ybuf[pl.ds(slot_ref[(dev * tok_dev + t) * top + k], sub), :]
                        acc = row if acc is None else acc + row
                    part[p, dev, pl.ds(t * sub, sub), :] = acc
                return 0
            lax.fori_loop(0, tok_dev // 8, one, 0)
            return 0
        lax.fori_loop(0, n_dev, dev_loop, 0)

    def chunk(c, _):
        down(c, 0, n_exp // 2)
        @pl.when(c >= 2)
        def _():
            on_first(c - 2)
        @pl.when(c >= 1)
        def _():
            on_core(c - 1)
        down(c, n_exp // 2, n_exp)
        @pl.when(c >= 2)
        def _():
            for cp in copy_core(c - 2):
                cp.wait_send()
        combine(c)
        for cp in copy_core(c):
            cp.start()
        return 0

    lax.fori_loop(0, n_chunk, chunk, 0)
    on_first(n_chunk - 2)
    on_core(n_chunk - 1)
    on_first(n_chunk - 1)

    def finish(c, _):
        on_second(c)
        for i in range(sub):
            at = pl.ds(pl.multiple_of(c * cw + i * LANES, LANES), LANES)
            routed = got_core[c, 2 * by + bx, pl.ds(i, tok_dev, stride=sub), :]
            out_ref[:, at] = (base_ref[:, at] + routed).astype(out_ref.dtype)
        for cp in copy_x(c) + copy_y(c) + copy_2(c):
            cp.wait_send()
        return 0
    lax.fori_loop(0, n_chunk, finish, 0)
    for c in (n_chunk - 2, n_chunk - 1):
        for cp in copy_core(c):
            cp.wait_send()


def down_reduce(slot_off, hidden, w_down, gate_col, base, cw=512):
    n_exp, cap, inter = hidden.shape
    tok_dev, d = base.shape
    sub, n_chunk = cw // LANES, d // cw
    blk = tok_dev * sub
    f32 = jnp.float32
    return pl.pallas_call(
        functools.partial(down_kernel, cw),
        out_shape=jax.ShapeDtypeStruct((tok_dev, d), jnp.bfloat16),
        in_specs=[
            pl.BlockSpec(memory_space=pltpu.SMEM),
            pl.BlockSpec(memory_space=pl.ANY),
            pl.BlockSpec(memory_space=pl.ANY),
            pl.BlockSpec(memory_space=pltpu.VMEM),
            pl.BlockSpec(memory_space=pltpu.VMEM),
        ],
        out_specs=pl.BlockSpec(memory_space=pltpu.VMEM),
        scratch_shapes=[
            pltpu.VMEM((n_exp, cap, inter), jnp.bfloat16),
            pltpu.VMEM((3, inter, cw), jnp.bfloat16),
            pltpu.VMEM((n_exp * cap * sub + 8, LANES), f32),
            pltpu.VMEM((2, 8, blk, LANES), f32),
            pltpu.VMEM((n_chunk, 4, blk, LANES), f32),
            pltpu.VMEM((n_chunk, 2, blk // 2, LANES), f32),
            pltpu.VMEM((n_chunk, 2, blk // 2, LANES), f32),
            pltpu.VMEM((n_chunk, blk // 2, LANES), f32),
            pltpu.VMEM((n_chunk, blk // 2, LANES), f32),
            pltpu.SemaphoreType.DMA((n_exp,)),
            pltpu.SemaphoreType.DMA((3,)),
            pltpu.SemaphoreType.DMA((2, 4)),
            pltpu.SemaphoreType.DMA((n_chunk, 4)),
            pltpu.SemaphoreType.DMA((n_chunk, 2)),
            pltpu.SemaphoreType.DMA((n_chunk, 2)),
            pltpu.SemaphoreType.DMA((n_chunk, 2)),
            pltpu.SemaphoreType.DMA((n_chunk, 2)),
            pltpu.SemaphoreType.DMA((n_chunk, 2)),
            pltpu.SemaphoreType.DMA((n_chunk, 2)),
        ],
        compiler_params=pltpu.CompilerParams(vmem_limit_bytes=VMEM_LIMIT, collective_id=1, has_side_effects=True),
        cost_estimate=pl.CostEstimate(flops=2 * n_exp * cap * d * inter, bytes_accessed=2 * n_exp * d * inter, transcendentals=0),
        name="down_reduce",
    )(slot_off, hidden, w_down, gate_col, base)


def solution(mesh):
    def local_block(hidden_in, norm_gain, router_w, w_gate, w_up, w_down, ws_gate, ws_up, ws_down, expert_ids):
        tok_dev, top_k = expert_ids.shape
        d = hidden_in.shape[1]
        n_exp = w_gate.shape[0]
        cap = 512
        sub = 4
        me = lax.axis_index("ep")
        x_norm = rms_norm(hidden_in, norm_gain)
        xn_all = lax.all_gather(x_norm, "ep", axis=0, tiled=True)
        gate_vals = route_gates(x_norm, router_w, expert_ids)
        ids_all = lax.all_gather(expert_ids, "ep", axis=0, tiled=True)
        gates_all = lax.all_gather(gate_vals, "ep", axis=0, tiled=True)
        shared_out = swiglu(x_norm, ws_gate, ws_up, ws_down)
        base = hidden_in.astype(jnp.float32) + shared_out.astype(jnp.float32)

        tokens = ids_all.shape[0]
        local = ids_all - me * n_exp
        hot = local[:, :, None] == jnp.arange(n_exp, dtype=jnp.int32)[None, None, :]
        hit = jnp.any(hot, axis=1)
        count = jnp.cumsum(hit.astype(jnp.int32), axis=0)
        slot = jnp.arange(n_exp, dtype=jnp.int32)[None, :] * cap + count - 1
        slot_off = jnp.sum(jnp.where(hot, slot[:, None, :], 0), axis=2)
        slot_off = jnp.where((local >= 0) & (local < n_exp), slot_off, n_exp * cap) * sub
        rank = jnp.arange(cap, dtype=jnp.int32)
        tok = jnp.sum((count.T[:, None, :] <= rank[None, :, None]).astype(jnp.int32), axis=2)
        tok_off = jnp.minimum(tok, tokens - 1).reshape(-1) * (d // LANES)
        gate_tok = jnp.sum(jnp.where(hot, gates_all[:, :, None], 0.0), axis=1)
        mine = (count.T[:, None, :] == rank[None, :, None] + 1) & hit.T[:, None, :]
        gate_col = jnp.sum(jnp.where(mine, gate_tok.T[:, None, :], 0.0), axis=2)[:, :, None]

        hidden = gate_up(tok_off, xn_all, w_gate, w_up)
        return down_reduce(slot_off.reshape(-1), hidden, w_down, gate_col, base)

    row_spec = P(("dp", "ep"), None)
    in_specs = (row_spec, P(), P(), P("ep"), P("ep"), P("ep"), P(), P(), P(), row_spec)
    return jax.shard_map(local_block, mesh=mesh, in_specs=in_specs, out_specs=row_spec, check_vma=False)
```

time: 907 us -> 324 us (0.36); the launches traced: 895 us -> 323 us
  waiting for transfers between devices: 404 us -> 0.02 us
  Pallas kernels: 0 us -> 230 us
  local copies, waits for them, and re-layouts: 200 us -> 7.12 us
  matrix products: 183 us -> 27.4 us
  other arithmetic: 93.7 us -> 18.3 us
  blocking collectives: 0 us -> 26.6 us
  starting transfers between devices: 14.3 us -> 0.01 us
  between operations: 0.85 us -> 13.5 us
    all_to_all x3 -> x0, waiting for transfers between devices: 404 us -> none  [the longest x1 209 us: local_block(): recv_rows = lax.all_to_all(send_rows, 'ep', 0, 0, tiled=True)]
    pallas_call x0 -> x2, Pallas kernels: none -> 230 us  [the longest x1 141 us: down_reduce(): pl.pallas_call(functools.partial(down_kernel, cw), out_shape=jax.ShapeDty...]
    gather x10 -> x0, local copies, waits for them, and re-layouts: 168 us -> none  [the longest x1 47.5 us: local_block(): jnp.take(recv_rows, buf_row, axis=0, mode='fill', fill_value=0)]
    dot_general x4 -> x0, matrix products: 163 us -> none  [the longest x1 56.1 us: expert_stack(): jnp.einsum('ecd,edi->eci', expert_in, w_up, preferred_element_type=jnp.fl...]
    select_n x8 -> x0, other arithmetic: 54.7 us -> none  [the longest x1 18.5 us: local_block(): jnp.take(expert_out, buf_slot, axis=0, mode='fill', fill_value=0)]
    scatter x3 -> x0, local copies, waits for them, and re-layouts: 28.5 us -> none  [the longest x1 15.5 us: local_block(): jnp.full((recv_cap,), recv_cap, jnp.int32).at[buf_slot]]
    all_gather x0 -> x2, blocking collectives: none -> 26.6 us  [the longest x1 14.6 us: local_block(): ids_all = lax.all_gather(expert_ids, 'ep', axis=0, tiled=True)]
    reduce_sum x3 -> x4, other arithmetic: 29.1 us -> 11 us  [the longest x1 6.91 us: local_block(): jnp.sum(jnp.where(mine, gate_tok.T[:, None, :], 0.0), axis=2)[:, :, None]]
  transfers between devices with their start and end apart: 3 -> 1, of which waited for: 2 -> 0; matrix products, arithmetic and copies ran while one was open for 12% -> 14% of each run, Pallas kernels for 0% -> 0%
where the time goes in v1:
time: 324 us; the launch traced here: 323 us
  Pallas kernels  230 us (71%)
  matrix products  27.4 us (8%)
  blocking collectives  26.6 us (8%)
  other arithmetic  18.3 us (6%)
  between operations  13.5 us (4%)
  local copies, waits for them, and re-layouts  7.12 us (2%)
    pallas_call x1, Pallas kernels, down_reduce(): pl.pallas_call(functools.partial(down_kernel, cw), out_shape=jax.ShapeDty...  141 us
    pallas_call x1, Pallas kernels, gate_up(): pl.pallas_call(gate_up_kernel, grid_spec=pltpu.PrefetchScalarGridSpec(num...  89.2 us
    dot_general x1, matrix products, swiglu(): jnp.dot(hidden, down_mat, preferred_element_type=jnp.float32)  16.5 us
    all_gather x1, blocking collectives, local_block(): ids_all = lax.all_gather(expert_ids, 'ep', axis=0, tiled=True)  14.6 us
    all_gather x1, blocking collectives, local_block(): gates_all = lax.all_gather(gate_vals, 'ep', axis=0, tiled=True)  12 us
    dot_general x1, matrix products, swiglu(): h_gate = jnp.dot(tok_rows, gate_mat, preferred_element_type=jnp.float32)  9.54 us
    reduce_sum x1, other arithmetic, local_block(): jnp.sum(jnp.where(mine, gate_tok.T[:, None, :], 0.0), axis=2)[:, :, None]  6.91 us
  transfers between devices with their start and end apart: 1, of which 0 were waited for; matrix products, arithmetic and copies ran while one was open for 14% of the time, Pallas kernels for 0%

profile of v1, /device:TPU:0, one launch (start us, length us, event | category | flops | bytes accessed | tf_op | source)
XLA Modules:
  0.0 323.4 jit_solution(5104125851430564040)
XLA Ops:
  6.5 0.0 copy-start
  6.5 0.0 all-gather.2.cloned.1.call-start
  6.5 1.7 fusion.2
  8.3 2.7 fusion.4
  11.0 0.0 all-gather.2.cloned.1.call-update
  11.1 0.0 copy-done.3
  11.1 14.6 %all_gather.9 = s32[2048,6]{0,1:T(8,128)S(1)} all-gather(s32[256,6]{0,1:T(8,128)S(1)} %copy-done.3), channel_id=1, replica_groups=mesh['dp'=1,'ep'=8] {'ep'}, dimensions={0}, use_global_device_ids=true | all-gather | bytes 55296 | tf_op jit(solution)/shard_map/all_gather | solution.py:320
  25.8 2.3 reduce-window.6
  28.0 0.3 slice_reduce_fusion
  28.3 0.2 reduce-window.9
  28.5 0.1 add_bitcast_fusion.1
  28.6 4.0 %convert_reduce_fusion = s32[8,512]{1,0:T(8,128)S(1)} fusion(s32[8,2048]{1,0:T(8,128)S(1)} %bitcast.24), kind=kLoop, calls=%fused_computation.1 | loop fusion | flops 25161728 | bytes 81920 | tf_op jit(solution)/shard_map/reduce_sum | solution.py:334
  32.6 0.6 copy.25
  33.2 0.1 add_bitcast_fusion
  33.3 0.1 select_reduce_fusion.4
  33.4 0.4 copy.22
  33.8 1.3 reshape.50.slot_ref
  35.1 0.0 copy-done
  35.1 0.0 copy-done.2
  35.1 0.0 copy-done.4
  35.1 1.4 fusion.7
  36.6 0.1 select_reduce_fusion.1
  36.7 12.0 %all_gather.11 = f32[2048,6]{0,1:T(8,128)S(1)} all-gather(f32[256,6]{0,1:T(8,128)S(1)} %multiply_divide_fusion), channel_id=1, replica_groups=mesh['dp'=1,'ep'=8] {'ep'}, dimensions={0}, use_global_device_ids=true | all-gather | bytes 55296 | tf_op jit(solution)/shard_map/all_gather | solution.py:321
  48.7 0.1 select_reduce_fusion.3
  48.8 6.9 %select_reduce_fusion = f32[8,512]{1,0:T(8,128)S(1)} fusion(f32[8,2048]{1,0:T(8,128)S(1)} %bitcast.23, s32[8,2048]{1,0:T(8,128)S(1)} %bitcast.25, s32[512]{0:T(512)S(1)} %iota_add_fusion, pred[8,2048]{1,0:T(8,128)(4,1)S(1)} %bitcast.26), kind=kLoop, calls=%fused_computation | loop fusion | flops 33550336 | bytes 165888 | tf_op jit(solution)/shard_map/reduce_sum | solution.py:338
  55.7 2.0 copy.23.gate_ref
  57.7 9.5 %fusion.12 = f32[256,3072]{1,0:T(8,128)} fusion(bf16[2560,3072]{1,0:T(8,128)(2,1)} %param.16, bf16[256,2560]{1,0:T(8,128)(2,1)S(1)} %copy-done.2, f32[2560]{0:T(1024)S(1)} %copy-done.4, f32[256]{0:T(256)S(1)} %add_rsqrt_fusion), kind=kOutput, calls=%fused_computation.37 | convolution fusion | flops 4029153280 | bytes 20196352 | tf_op jit(solution)/shard_map/dot_general | solution.py:32
  67.2 16.5 %convert_add_fusion.base_ref = f32[256,2560]{1,0:T(8,128)} fusion(bf16[256,2560]{1,0:T(8,128)(2,1)S(1)} %copy-done.2, bf16[3072,2560]{1,0:T(8,128)(2,1)} %param.18, bf16[2560,3072]{1,0:T(8,128)(2,1)} %param.17, f32[256,3072]{1,0:T(8,128)} %fusion.12, f32[2560]{0:T(1024)S(1)} %copy-done.4, f32[256]{0:T(256)S(1)} %add_rsqrt_fusion), kind=kOutput, calls=%fused_computation.4 | convolution fusion | flops 8063025152 | bytes 38546432 | tf_op jit(solution)/shard_map/dot_general | solution.py:35
  83.7 89.2 %gate_up.1.h_hbm = bf16[8,512,1536]{2,1,0:T(8,128)(2,1)} custom-call(s32[4096]{0:T(1024)} %bitcast.29, bf16[2048,2560]{1,0:T(8,128)(2,1)} %all-gather.2.cloned.1.call-done.xn_ref, bf16[8,2560,1536]{2,1,0:T(8,128)(2,1)} %wg_ref.1, bf16[8,2560,1536]{2,1,0:T(8,128)(2,1)} %wu_ref.1), custom_call_target="tpu_custom_call" | custom-call | flops 64424509440 | bytes 125829120 | tf_op jit(solution)/shard_map/gate_up/pallas_call | solution.py:79
  172.9 141.2 %down_reduce.1 = bf16[256,2560]{1,0:T(8,128)(2,1)} custom-call(s32[12288]{0:T(1024)} %reshape.50.slot_ref, bf16[8,512,1536]{2,1,0:T(8,128)(2,1)} %gate_up.1.h_hbm, bf16[8,1536,2560]{2,1,0:T(8,128)(2,1)} %wd_hbm.1, f32[8,512,1]{2,1,0:T(8,128)} %copy.23.gate_ref, f32[256,2560]{1,0:T(8,128)} %convert_add_fusion.base_ref), custom_call_target="tpu_custom_call" | custom-call | flops 32212254720 | bytes 62914560 | tf_op jit(solution)/shard_map/down_reduce/pallas_call | solution.py:271
  314.1 2.5 copy.31
  316.6 0.0 copy-done.1
  (16 shorter events, 0.2 us)
Async XLA Ops:
  6.5 28.6 %copy-start = (f32[64,2560]{1,0:T(8,128)S(1)}, f32[64,2560]{1,0:T(8,128)}, u32[]{:S(2)}) copy-start(f32[64,2560]{1,0:T(8,128)} %param.12) | copy-start | bytes 1966084
  6.5 4.5 %copy-start.3 = (s32[256,6]{0,1:T(8,128)S(1)}, s32[256,6]{0,1:T(8,128)}, u32[]{:S(2)}) copy-start(s32[256,6]{0,1:T(8,128)} %param.19) | copy-start | bytes 18436
  6.5 77.2 %all-gather.2.cloned.1.call-start = ((), (), s32[]{:S(2)}) async-start(), calls=%async_computation | async-start | bytes 11796480 | tf_op jit(solution)/shard_map/all_gather | solution.py:318
  11.0 24.1 %copy-start.2 = (bf16[256,2560]{1,0:T(8,128)(2,1)S(1)}, bf16[256,2560]{1,0:T(8,128)(2,1)}, u32[]{:S(2)}) copy-start(bf16[256,2560]{1,0:T(8,128)(2,1)} %param.10) | copy-start | bytes 3932164
  11.0 24.1 %copy-start.4 = (f32[2560]{0:T(1024)S(1)}, f32[2560]{0:T(1024)}, u32[]{:S(2)}) copy-start(f32[2560]{0:T(1024)} %param.11) | copy-start | bytes 30724
  172.9 143.7 %copy-start.1 = (f32[64,2560]{1,0:T(8,128)S(1)}, f32[64,2560]{1,0:T(8,128)}, u32[]{:S(2)}) copy-start(f32[64,2560]{1,0:T(8,128)} %param.12) | copy-start | bytes 1966084
Sparse Core Ops, SparseCore 0:
  11.2 61.0 all-gather.1

commit v2 on v1

v2 whole, which is shorter than its diff:
```python
import functools

import jax
import jax.numpy as jnp
from jax import lax
from jax.experimental import pallas as pl
from jax.experimental.pallas import tpu as pltpu
from jax.sharding import PartitionSpec as P

NORM_EPS = 1e-6
ROUTE_SCALE = 2.5
TOP = 6
WIDTHS = (768, 768, 768, 256)
SUB = 6
LANES = 128
MESH = pl.DeviceIdType.MESH
VMEM_LIMIT = 66_000_000


def neighbours():
    me = lax.axis_index("ep")
    core, bx, by = lax.rem(me, 2), lax.rem(me // 2, 2), me // 4
    return core, bx, by, me + 1 - 2 * core, me + 2 - 4 * bx, me + 4 - 8 * by


def gather_kernel(x_ref, gain_ref, rw_ref, ids_ref, wsg_hbm, wsu_hbm, wsd_hbm,
                  xn_all, base_ref, tok_ref, slot_ref, gcol_ref,
                  xn, wsg, wsu, wsd, hid, ids_all, gates_all, cnt, gtok, cnt3, gtok3,
                  w_sem, own_sem, meta_send, meta_recv, snd, rcv):
    tok_dev, d = x_ref.shape
    n_dev, top_pad = ids_all.shape[0], ids_all.shape[1]
    n_exp, tokens = cnt.shape
    cap = tok_ref.shape[2]
    half = tok_dev // 2
    ng, cg = wsg.shape[0], wsg.shape[2]
    nd, cd = wsd.shape[0], wsd.shape[2]
    core, bx, by, partner, xdev, ydev = neighbours()
    me = lax.axis_index("ep")
    diag = n_dev - 2 - (me - core) + core

    barrier = pltpu.get_barrier_semaphore()
    for j in range(1, n_dev):
        pl.semaphore_signal(barrier, inc=1, device_id={"ep": lax.rem(me + j, n_dev)}, device_id_type=MESH)

    def w_copies(c):
        at = pl.ds(pl.multiple_of(c * cg, LANES), cg)
        return [pltpu.make_async_copy(wsg_hbm.at[:, at], wsg.at[c], w_sem.at[0, c]), pltpu.make_async_copy(wsu_hbm.at[:, at], wsu.at[c], w_sem.at[1, c])]

    def d_copy(c):
        return pltpu.make_async_copy(wsd_hbm.at[:, pl.ds(pl.multiple_of(c * cd, LANES), cd)], wsd.at[c], w_sem.at[2, c])

    for c in range(ng):
        for cp in w_copies(c):
            cp.start()
    for c in range(nd):
        d_copy(c).start()

    def norm(b, _):
        at = pl.ds(pl.multiple_of(b * 16, 16), 16)
        x = x_ref[at, :].astype(jnp.float32)
        inv = lax.rsqrt(jnp.mean(x * x, axis=1, keepdims=True) + NORM_EPS)
        xn[at, :] = (x * inv * gain_ref[...]).astype(jnp.bfloat16)
        return 0
    lax.fori_loop(0, tok_dev // 16, norm, 0)

    pl.semaphore_wait(barrier, n_dev - 1)

    def remote(src, dst, k, dev):
        return pltpu.make_async_remote_copy(src_ref=src, dst_ref=dst, send_sem=snd.at[k], recv_sem=rcv.at[k], device_id={"ep": dev}, device_id_type=MESH)

    def rows(dev, h):
        return pl.ds(pl.multiple_of(dev * tok_dev + h * half, half), half)

    def mine(k, h, dev):
        return remote(xn.at[pl.ds(h * half, half)], xn_all.at[rows(me, h)], k, dev)

    def pass_on(k, src, h, dev):
        return remote(xn_all.at[rows(src, h)], xn_all.at[rows(src, h)], k, dev)

    own = pltpu.make_async_copy(xn, xn_all.at[pl.ds(pl.multiple_of(me * tok_dev, tok_dev), tok_dev)], own_sem)
    own.start()
    direct = [mine(0, 0, xdev), mine(1, 1, ydev), mine(2, 1, xdev), mine(3, 0, ydev), mine(4, 0, partner), mine(5, 1, partner)]
    for cp in direct:
        cp.start()

    def meta(j, which):
        ref = (ids_all, gates_all)[which]
        src = (ids_ref, gates_all.at[me])[which]
        dev = lax.rem(me + j, n_dev)
        return pltpu.make_async_remote_copy(src_ref=src, dst_ref=ref.at[me], send_sem=meta_send.at[which, j], recv_sem=meta_recv.at[which, j], device_id={"ep": dev}, device_id_type=MESH)

    for j in range(1, n_dev):
        meta(j, 0).start()
    ids_all[me] = ids_ref[...]

    logits = lax.dot_general(rw_ref[...], xn[...].astype(jnp.float32), (((1,), (1,)), ((), ())), precision=lax.Precision.HIGHEST, preferred_element_type=jnp.float32)
    scores = jax.nn.sigmoid(logits)
    names = lax.broadcasted_iota(jnp.int32, scores.shape, 0)
    picked = []
    for k in range(TOP):
        picked.append(jnp.sum(jnp.where(names == ids_ref[k:k + 1, :], scores, 0.0), axis=0, keepdims=True))
    total = picked[0]
    for k in range(1, TOP):
        total = total + picked[k]
    for k in range(TOP):
        gates_all[me, k:k + 1, :] = ROUTE_SCALE * picked[k] / total
    gates_all[me, TOP:top_pad, :] = jnp.zeros((top_pad - TOP, tok_dev), jnp.float32)
    for j in range(1, n_dev):
        meta(j, 1).start()

    def shared_up(c, _):
        for cp in w_copies(c):
            cp.wait()
        g = jnp.dot(xn[...], wsg[c], preferred_element_type=jnp.float32)
        u = jnp.dot(xn[...], wsu[c], preferred_element_type=jnp.float32)
        hid[:, pl.ds(pl.multiple_of(c * cg, LANES), cg)] = (g * jax.nn.sigmoid(g) * u).astype(jnp.bfloat16)
        return 0
    lax.fori_loop(0, ng, shared_up, 0)

    def shared_down(c, _):
        d_copy(c).wait()
        y = jnp.dot(hid[...], wsd[c], preferred_element_type=jnp.float32).astype(jnp.bfloat16)
        at = pl.ds(pl.multiple_of(c * cd, LANES), cd)
        base_ref[:, at] = x_ref[:, at].astype(jnp.float32) + y.astype(jnp.float32)
        return 0
    lax.fori_loop(0, nd, shared_down, 0)

    mine(0, 0, xdev).wait_recv()
    relay = [pass_on(6, xdev, 0, ydev)]
    relay[0].start()
    mine(1, 1, ydev).wait_recv()
    relay.append(pass_on(7, ydev, 1, xdev))
    relay[1].start()
    side = [pass_on(8, xdev, 0, partner), pass_on(9, ydev, 1, partner)]
    for cp in side:
        cp.start()

    for which in range(2):
        for j in range(1, n_dev):
            meta(j, which).wait_recv()

    def hits(dev, _):
        at = pl.ds(pl.multiple_of(dev * tok_dev, tok_dev), tok_dev)
        ids = ids_all[dev]
        gates = gates_all[dev]
        for e in range(n_exp):
            hot = ids == me * n_exp + e
            cnt[e:e + 1, at] = jnp.sum(jnp.where(hot, 1.0, 0.0), axis=0, keepdims=True)
            gtok[e:e + 1, at] = jnp.sum(jnp.where(hot, gates, 0.0), axis=0, keepdims=True)
        return 0
    lax.fori_loop(0, n_dev, hits, 0)

    upper = (lax.broadcasted_iota(jnp.int32, (LANES, LANES), 0) <= lax.broadcasted_iota(jnp.int32, (LANES, LANES), 1)).astype(jnp.float32).astype(jnp.bfloat16)
    run = jnp.zeros((n_exp, 1), jnp.float32)
    for i in range(tokens // LANES):
        at = slice(i * LANES, (i + 1) * LANES)
        hit = cnt[:, at]
        ranks = jnp.dot(hit.astype(jnp.bfloat16), upper, preferred_element_type=jnp.float32) + run
        run = ranks[:, LANES - 1:LANES]
        cnt[:, at] = ranks
        gate = jnp.where(hit > 0.0, gtok[:, at], 0.0)
        for e in range(n_exp):
            cnt3[e, :, at] = ranks[e:e + 1, :]
            gtok3[e, :, at] = gate[e:e + 1, :]

    def slots(dev, _):
        at = pl.ds(pl.multiple_of(dev * tok_dev, tok_dev), tok_dev)
        ids = ids_all[dev]
        slot = jnp.full(ids.shape, n_exp * cap, jnp.int32)
        for e in range(n_exp):
            slot = jnp.where(ids == me * n_exp + e, cnt[e:e + 1, at].astype(jnp.int32) + (e * cap - 1), slot)
        slot_ref[pl.ds(pl.multiple_of(dev * top_pad, top_pad), top_pad), :] = slot * SUB
        return 0
    lax.fori_loop(0, n_dev, slots, 0)

    mine(2, 1, xdev).wait_recv()
    mine(3, 0, ydev).wait_recv()
    more = [pass_on(10, xdev, 1, partner), pass_on(11, ydev, 0, partner)]
    for cp in more:
        cp.start()

    rb = 64
    eye = (lax.broadcasted_iota(jnp.int32, (LANES, LANES), 0) == lax.broadcasted_iota(jnp.int32, (LANES, LANES), 1))

    def table(e, _):
        for r0 in range(0, cap, LANES):
            cols = []
            for q in range(0, LANES, rb):
                rank = lax.broadcasted_iota(jnp.int32, (rb, LANES), 0).astype(jnp.float32) + float(r0 + q)
                before = jnp.zeros((rb, LANES), jnp.float32)
                gate = jnp.zeros((rb, LANES), jnp.float32)
                for i in range(tokens // LANES):
                    at = slice(i * LANES, (i + 1) * LANES)
                    c = cnt3[e, :, at]
                    before = before + jnp.where(c <= rank, 1.0, 0.0)
                    gate = gate + jnp.where(c == rank + 1.0, gtok3[e, :, at], 0.0)
                cols.append(jnp.sum(before, axis=1, keepdims=True))
                gcol_ref[e, r0 + q:r0 + q + rb, :] = jnp.broadcast_to(jnp.sum(gate, axis=1, keepdims=True), (rb, LANES))
            col = jnp.concatenate(cols, axis=0)
            row = jnp.sum(jnp.where(eye, col, 0.0), axis=0, keepdims=True)
            tok_ref[e, :, r0:r0 + LANES] = jnp.minimum(row, float(tokens - 1)).astype(jnp.int32) * (d // LANES)
        return 0
    lax.fori_loop(0, n_exp, table, 0)

    pass_on(6, diag, 0, ydev).wait_recv()
    last = [pass_on(12, diag, 0, partner)]
    last[0].start()
    pass_on(7, diag, 1, xdev).wait_recv()
    last.append(pass_on(13, diag, 1, partner))
    last[1].start()

    own.wait()
    for cp in direct + relay + side + more + last:
        cp.wait_send()
    for which in range(2):
        for j in range(1, n_dev):
            meta(j, which).wait_send()
    for k in (4, 5, 8, 9, 10, 11, 12, 13):
        mine(k, 0, partner).wait_recv()


def gather_rows(x, gain, router_w, ids_t, ws_gate, ws_up, ws_down, n_dev, n_exp, cap, cg=512, cd=512):
    tok_dev, d = x.shape
    inter = ws_gate.shape[1]
    tokens, top_pad = n_dev * tok_dev, ids_t.shape[0]
    f32, i32, bf16 = jnp.float32, jnp.int32, jnp.bfloat16
    vmem = pl.BlockSpec(memory_space=pltpu.VMEM)
    hbm = pl.BlockSpec(memory_space=pl.ANY)
    return pl.pallas_call(
        gather_kernel,
        out_shape=(
            jax.ShapeDtypeStruct((tokens, d), bf16),
            jax.ShapeDtypeStruct((tok_dev, d), f32),
            jax.ShapeDtypeStruct((n_exp, 1, cap), i32),
            jax.ShapeDtypeStruct((n_dev * top_pad, tok_dev), i32),
            jax.ShapeDtypeStruct((n_exp, cap, LANES), f32),
        ),
        in_specs=[vmem, vmem, vmem, vmem, hbm, hbm, hbm],
        out_specs=(hbm, vmem, vmem, vmem, vmem),
        scratch_shapes=[
            pltpu.VMEM((tok_dev, d), bf16),
            pltpu.VMEM((inter // cg, d, cg), bf16),
            pltpu.VMEM((inter // cg, d, cg), bf16),
            pltpu.VMEM((d // cd, inter, cd), bf16),
            pltpu.VMEM((tok_dev, inter), bf16),
            pltpu.VMEM((n_dev, top_pad, tok_dev), i32),
            pltpu.VMEM((n_dev, top_pad, tok_dev), f32),
            pltpu.VMEM((n_exp, tokens), f32),
            pltpu.VMEM((n_exp, tokens), f32),
            pltpu.VMEM((n_exp, 1, tokens), f32),
            pltpu.VMEM((n_exp, 1, tokens), f32),
            pltpu.SemaphoreType.DMA((3, max(inter // cg, d // cd))),
            pltpu.SemaphoreType.DMA,
            pltpu.SemaphoreType.DMA((2, n_dev)),
            pltpu.SemaphoreType.DMA((2, n_dev)),
            pltpu.SemaphoreType.DMA((14,)),
            pltpu.SemaphoreType.DMA((14,)),
        ],
        compiler_params=pltpu.CompilerParams(vmem_limit_bytes=VMEM_LIMIT, collective_id=2, has_side_effects=True),
        cost_estimate=pl.CostEstimate(flops=6 * tok_dev * d * inter, bytes_accessed=6 * d * inter, transcendentals=0),
        name="gather_rows",
    )(x, gain, router_w, ids_t, ws_gate, ws_up, ws_down)


def gate_up_kernel(tok_ref, xn_ref, wg_ref, wu_ref, h_ref, xf, gbuf, lhs):
    e = pl.program_id(0)
    j = pl.program_id(1)
    cap, d = lhs.shape
    nc = d // LANES

    @pl.when((e == 0) & (j == 0))
    def _():
        def widen(b, _):
            rows = pl.multiple_of(b * 64, 64)
            blk = xn_ref[pl.ds(rows, 64), :].astype(jnp.float32)
            for c in range(nc):
                xf[pl.ds(rows * nc + c, 64, stride=nc), :] = blk[:, c * LANES:(c + 1) * LANES]
            return 0
        lax.fori_loop(0, xn_ref.shape[0] // 64, widen, 0)

    @pl.when(j == 0)
    def _():
        def gather(b, _):
            for u in range(16):
                r = b * 16 + u
                gbuf[pl.ds(r * nc, nc), :] = xf[pl.ds(tok_ref[e * cap + r], nc), :]
            return 0
        lax.fori_loop(0, cap // 16, gather, 0)

        def narrow(b, _):
            rows = pl.multiple_of(b * 64, 64)
            for c in range(nc):
                lhs[pl.ds(rows, 64), c * LANES:(c + 1) * LANES] = gbuf[pl.ds(rows * nc + c, 64, stride=nc), :].astype(jnp.bfloat16)
            return 0
        lax.fori_loop(0, cap // 64, narrow, 0)

    g = jnp.dot(lhs[...], wg_ref[0], preferred_element_type=jnp.float32)
    u = jnp.dot(lhs[...], wu_ref[0], preferred_element_type=jnp.float32)
    h_ref[0] = (g * jax.nn.sigmoid(g) * u).astype(jnp.bfloat16)


def gate_up(tok_off, xn_all, w_gate, w_up, block=512):
    n_exp, d, inter = w_gate.shape
    cap = tok_off.shape[0] // n_exp
    tokens = xn_all.shape[0]
    return pl.pallas_call(
        gate_up_kernel,
        grid_spec=pltpu.PrefetchScalarGridSpec(
            num_scalar_prefetch=1,
            grid=(n_exp, inter // block),
            in_specs=[
                pl.BlockSpec((tokens, d), lambda e, j, t: (0, 0), pipeline_mode=pl.Buffered(1)),
                pl.BlockSpec((1, d, block), lambda e, j, t: (e, 0, j)),
                pl.BlockSpec((1, d, block), lambda e, j, t: (e, 0, j)),
            ],
            out_specs=pl.BlockSpec((1, cap, block), lambda e, j, t: (e, 0, j)),
            scratch_shapes=[
                pltpu.VMEM((tokens * d // LANES, LANES), jnp.float32),
                pltpu.VMEM((cap * d // LANES, LANES), jnp.float32),
                pltpu.VMEM((cap, d), jnp.bfloat16),
            ],
        ),
        out_shape=jax.ShapeDtypeStruct((n_exp, cap, inter), jnp.bfloat16),
        compiler_params=pltpu.CompilerParams(vmem_limit_bytes=VMEM_LIMIT, dimension_semantics=("arbitrary", "arbitrary")),
        cost_estimate=pl.CostEstimate(flops=4 * n_exp * cap * d * inter, bytes_accessed=4 * n_exp * d * inter, transcendentals=0),
        name="gate_up",
    )(tok_off, xn_all, w_gate, w_up)


def down_kernel(slot_ref, h_hbm, wd_hbm, gate_ref, out_ref,
                h, wd, ybuf, part, sums, got_x, got_y, got_2,
                h_sem, wd_sem, send_core, recv_core, send_x, recv_x, send_y, recv_y, send_2, recv_2):
    n_exp, cap, inter = h.shape
    tok_dev = out_ref.shape[0]
    half = tok_dev // 2
    core, bx, by, partner, xdev, ydev = neighbours()
    chip_d, chip_x, chip_y, chip_o = 2 * (1 - by) + 1 - bx, 2 * by + 1 - bx, 2 * (1 - by) + bx, 2 * by + bx
    chips = (chip_d, chip_x, chip_y, chip_o)
    subs = [w // LANES for w in WIDTHS]
    offs = [sum(subs[:c]) for c in range(len(subs))]

    barrier = pltpu.get_barrier_semaphore()
    for dev in (partner, xdev, ydev):
        pl.semaphore_signal(barrier, inc=1, device_id={"ep": dev}, device_id_type=MESH)

    def h_copy(e):
        return pltpu.make_async_copy(h_hbm.at[e], h.at[e], h_sem.at[e])

    def wd_copy(c, e):
        slot = lax.rem(c * n_exp + e, 3)
        return pltpu.make_async_copy(wd_hbm.at[e, :, pl.ds(offs[c] * LANES, WIDTHS[c])], wd.at[slot, :, pl.ds(0, WIDTHS[c])], wd_sem.at[slot])

    h_copy(0).start()
    wd_copy(0, 0).start()
    wd_copy(0, 1).start()
    for e in range(1, n_exp):
        h_copy(e).start()
    ybuf[pl.ds(n_exp * cap * SUB, 8), :] = jnp.zeros((8, LANES), jnp.float32)
    pl.semaphore_wait(barrier, 3)

    def remote(src, dst, send, recv, dev):
        return pltpu.make_async_remote_copy(src_ref=src, dst_ref=dst, send_sem=send, recv_sem=recv, device_id={"ep": dev}, device_id_type=MESH)

    def full(c):
        return pl.ds(offs[c] * tok_dev, subs[c] * tok_dev)

    def low(c):
        return pl.ds(offs[c] * tok_dev, subs[c] * half)

    def high(c):
        return pl.ds(offs[c] * tok_dev + subs[c] * half, subs[c] * half)

    def land(c):
        return pl.ds(offs[c] * half, subs[c] * half)

    def core_copy(c, i):
        return remote(part.at[2 * chips[i] + 1 - core, pl.ds(0, subs[c] * tok_dev)], sums.at[chips[i], full(c)], send_core.at[c, i], recv_core.at[c, i], partner)

    def x_copy(c, i):
        return remote(sums.at[(chip_d, chip_x)[i], low(c)], got_x.at[i, land(c)], send_x.at[c, i], recv_x.at[c, i], xdev)

    def y_copy(c, i):
        return remote(sums.at[(chip_d, chip_y)[i], high(c)], got_y.at[i, land(c)], send_y.at[c, i], recv_y.at[c, i], ydev)

    def hop_copy(c, i):
        if i == 0:
            return remote(sums.at[chip_y, low(c)], got_2.at[0, land(c)], send_2.at[c, 0], recv_2.at[c, 0], ydev)
        return remote(sums.at[chip_x, high(c)], got_2.at[1, land(c)], send_2.at[c, 1], recv_2.at[c, 1], xdev)

    def add_into(dst, src, n):
        def one(i, _):
            at = pl.ds(pl.multiple_of(i * 128, 128), 128)
            dst[at, :] = dst[at, :] + src[at, :]
            return 0
        lax.fori_loop(0, n // 128, one, 0)

    def on_core(c, i):
        core_copy(c, i).wait_recv()
        add_into(sums.at[chips[i], full(c)], part.at[2 * chips[i] + core, pl.ds(0, subs[c] * tok_dev)], subs[c] * tok_dev)
        if i == 0:
            x_copy(c, 0).start()
            y_copy(c, 0).start()
        elif i == 1:
            x_copy(c, 1).start()
        elif i == 2:
            y_copy(c, 1).start()

    def on_first(c):
        x_copy(c, 0).wait_recv()
        add_into(sums.at[chip_y, low(c)], got_x.at[0, land(c)], subs[c] * half)
        hop_copy(c, 0).start()
        y_copy(c, 0).wait_recv()
        add_into(sums.at[chip_x, high(c)], got_y.at[0, land(c)], subs[c] * half)
        hop_copy(c, 1).start()

    def on_own(c):
        x_copy(c, 1).wait_recv()
        add_into(sums.at[chip_o, low(c)], got_x.at[1, land(c)], subs[c] * half)
        y_copy(c, 1).wait_recv()
        add_into(sums.at[chip_o, high(c)], got_y.at[1, land(c)], subs[c] * half)

    def finish(c):
        hop_copy(c, 0).wait_recv()
        add_into(sums.at[chip_o, low(c)], got_2.at[0, land(c)], subs[c] * half)
        hop_copy(c, 1).wait_recv()
        add_into(sums.at[chip_o, high(c)], got_2.at[1, land(c)], subs[c] * half)
        for i in range(subs[c]):
            at = (offs[c] + i) * LANES
            out_ref[:, at:at + LANES] = sums[chip_o, pl.ds(offs[c] * tok_dev + i, tok_dev, stride=subs[c]), :]

    def down(c, lo, hi):
        width = WIDTHS[c]

        def one(e, _):
            slot = lax.rem(c * n_exp + e, 3)
            @pl.when(e + 2 < n_exp)
            def _():
                wd_copy(c, e + 2).start()
            if c + 1 < len(WIDTHS):
                @pl.when(e + 2 >= n_exp)
                def _():
                    wd_copy(c + 1, e + 2 - n_exp).start()
            if c == 0:
                h_copy(e).wait()
            wd_copy(c, e).wait()
            y = jnp.dot(h[e], wd[slot, :, 0:width], preferred_element_type=jnp.float32)
            y = y.astype(jnp.bfloat16).astype(jnp.float32)
            gate = gate_ref[e]
            for i in range(subs[c]):
                ybuf[pl.ds(e * (cap * SUB) + i, cap, stride=SUB), :] = y[:, i * LANES:(i + 1) * LANES] * gate
            return 0
        lax.fori_loop(lo, hi, one, 0)

    def combine(c, i):
        sub = subs[c]

        def one_dev(j, _):
            dev = 2 * chips[i] + j

            def one(b, _):
                at = dev * (8 * tok_dev) + b * 8
                for u in range(8):
                    acc = ybuf[pl.ds(slot_ref[at + u], sub), :]
                    for k in range(1, TOP):
                        acc = acc + ybuf[pl.ds(slot_ref[at + (k * tok_dev + u)], sub), :]
                    part[dev, pl.ds(b * (8 * sub) + u * sub, sub), :] = acc
                return 0
            lax.fori_loop(0, tok_dev // 8, one, 0)
            return 0
        lax.fori_loop(0, 2, one_dev, 0)

    last = len(WIDTHS) - 1
    for c in range(len(WIDTHS)):
        down(c, 0, 1)
        if c >= 1:
            on_core(c - 1, 3)
        down(c, 1, n_exp // 2)
        if c >= 1:
            on_first(c - 1)
        down(c, n_exp // 2, n_exp)
        if c >= 2:
            on_own(c - 2)
            finish(c - 2)
        for i in range(4):
            if c >= 1:
                core_copy(c - 1, i).wait_send()
            combine(c, i)
            core_copy(c, i).start()
            if i >= 1:
                on_core(c, i - 1)
    on_core(last, 3)
    on_first(last)
    on_own(last - 1)
    finish(last - 1)
    on_own(last)
    finish(last)
    for c in range(len(WIDTHS)):
        for i in range(2):
            x_copy(c, i).wait_send()
            y_copy(c, i).wait_send()
            hop_copy(c, i).wait_send()
    for i in range(4):
        core_copy(last, i).wait_send()


def down_reduce(slot_off, hidden, w_down, gate_col, tok_dev):
    n_exp, cap, inter = hidden.shape
    d = w_down.shape[2]
    n_chunk = len(WIDTHS)
    rows = tok_dev * d // LANES
    f32 = jnp.float32
    return pl.pallas_call(
        down_kernel,
        out_shape=jax.ShapeDtypeStruct((tok_dev, d), f32),
        in_specs=[
            pl.BlockSpec(memory_space=pltpu.SMEM),
            pl.BlockSpec(memory_space=pl.ANY),
            pl.BlockSpec(memory_space=pl.ANY),
            pl.BlockSpec(memory_space=pltpu.VMEM),
        ],
        out_specs=pl.BlockSpec(memory_space=pltpu.VMEM),
        scratch_shapes=[
            pltpu.VMEM((n_exp, cap, inter), jnp.bfloat16),
            pltpu.VMEM((3, inter, max(WIDTHS)), jnp.bfloat16),
            pltpu.VMEM((n_exp * cap * SUB + 8, LANES), f32),
            pltpu.VMEM((8, tok_dev * SUB, LANES), f32),
            pltpu.VMEM((4, rows, LANES), f32),
            pltpu.VMEM((2, rows // 2, LANES), f32),
            pltpu.VMEM((2, rows // 2, LANES), f32),
            pltpu.VMEM((2, rows // 2, LANES), f32),
            pltpu.SemaphoreType.DMA((n_exp,)),
            pltpu.SemaphoreType.DMA((3,)),
            pltpu.SemaphoreType.DMA((n_chunk, 4)),
            pltpu.SemaphoreType.DMA((n_chunk, 4)),
            pltpu.SemaphoreType.DMA((n_chunk, 2)),
            pltpu.SemaphoreType.DMA((n_chunk, 2)),
            pltpu.SemaphoreType.DMA((n_chunk, 2)),
            pltpu.SemaphoreType.DMA((n_chunk, 2)),
            pltpu.SemaphoreType.DMA((n_chunk, 2)),
            pltpu.SemaphoreType.DMA((n_chunk, 2)),
        ],
        compiler_params=pltpu.CompilerParams(vmem_limit_bytes=VMEM_LIMIT, collective_id=1, has_side_effects=True),
        cost_estimate=pl.CostEstimate(flops=2 * n_exp * cap * d * inter, bytes_accessed=2 * n_exp * d * inter, transcendentals=0),
        name="down_reduce",
    )(slot_off, hidden, w_down, gate_col)


def solution(mesh):
    n_dev = mesh.shape["ep"]

    def local_block(hidden_in, norm_gain, router_w, w_gate, w_up, w_down, ws_gate, ws_up, ws_down, expert_ids):
        n_exp = w_gate.shape[0]
        cap = 512
        ids_t = jnp.pad(expert_ids.T, ((0, 8 - TOP), (0, 0)), constant_values=-1)
        xn_all, base, tok_off, slots, gate_col = gather_rows(hidden_in, norm_gain[None, :], router_w, ids_t, ws_gate, ws_up, ws_down, n_dev, n_exp, cap)
        hidden = gate_up(tok_off.reshape(-1), xn_all, w_gate, w_up)
        routed = down_reduce(slots.reshape(-1), hidden, w_down, gate_col, hidden_in.shape[0])
        return (base + routed).astype(jnp.bfloat16)

    row_spec = P(("dp", "ep"), None)
    in_specs = (row_spec, P(), P(), P("ep"), P("ep"), P("ep"), P(), P(), P(), row_spec)
    return jax.shard_map(local_block, mesh=mesh, in_specs=in_specs, out_specs=row_spec, check_vma=False)
```

time: 324 us -> 267 us (0.82)
  Pallas kernels: 230 us -> 259 us
  matrix products: 27.4 us -> 0 us
  blocking collectives: 26.6 us -> 0 us
  other arithmetic: 18.3 us -> 3.88 us
  between operations: 13.5 us -> 0.02 us
    pallas_call x1 -> x2, Pallas kernels: 141 us -> 170 us  [the longest x1 113 us: down_reduce(): pl.pallas_call(down_kernel, out_shape=jax.ShapeDtypeStruct((tok_dev, d),...]
    dot_general x3 -> x0, matrix products: 27.4 us -> none  [the longest x1 16.5 us: swiglu(): jnp.dot(hidden, down_mat, preferred_element_type=jnp.float32)]
    all_gather x2 -> x0, blocking collectives: 26.6 us -> none  [the longest x1 14.6 us: local_block(): ids_all = lax.all_gather(expert_ids, 'ep', axis=0, tiled=True)]
    reduce_sum x6 -> x0, other arithmetic: 12.9 us -> none  [the longest x1 6.91 us: local_block(): jnp.sum(jnp.where(mine, gate_tok.T[:, None, :], 0.0), axis=2)[:, :, None]]
  transfers between devices with their start and end apart: 1 -> 0, of which waited for: 0 -> 0; matrix products, arithmetic and copies ran while one was open for 14% -> 0% of each run, Pallas kernels for 0% -> 0%
where the time goes in v2:
time: 267 us
  Pallas kernels  259 us (97%)
  local copies, waits for them, and re-layouts  4.11 us (2%)
  other arithmetic  3.88 us (1%)
    pallas_call x1, Pallas kernels, down_reduce(): pl.pallas_call(down_kernel, out_shape=jax.ShapeDtypeStruct((tok_dev, d),...  113 us
    pallas_call x1, Pallas kernels, gate_up(): pl.pallas_call(gate_up_kernel, grid_spec=pltpu.PrefetchScalarGridSpec(num...  89.2 us
    pallas_call x1, Pallas kernels, gather_rows(): pl.pallas_call(gather_kernel, out_shape=(jax.ShapeDtypeStruct((tokens, d)...  56.7 us

profile of v2, /device:TPU:0, one launch (start us, length us, event | category | flops | bytes accessed | tf_op | source)
XLA Modules:
  0.0 266.9 jit_solution(4377369881291397019)
XLA Ops:
  0.0 1.3 pad.4.ids_ref
  1.3 1.3 broadcast_in_dim.3.gain_ref
  2.6 56.7 %gather_rows.1 = (bf16[2048,2560]{1,0:T(8,128)(2,1)}, f32[256,2560]{1,0:T(8,128)}, s32[8,1,512]{2,1,0:T(1,128)}, s32[64,256]{1,0:T(8,128)}, f32[8,512,128]{2,1,0:T(8,128)}) custom-call(bf16[256,2560]{1,0:T(8,128)(2,1)} %x_ref.1, f32[1,2560]{1,0:T(1,128)} %broadcast_in_dim.3.gain_ref, f32[64,2560]{1,0:T(8,128)} %rw_ref.1, s32[8,256]{1,0:T(8,128)} %pad.4.ids_ref, ...), custom_call_target="tpu_custom_call" | custom-call | flops 12079595520 | bytes 47185920 | tf_op jit(solution)/shard_map/gather_rows/pallas_call | solution.py:229
  59.3 1.5 copy.11
  60.8 89.2 %gate_up.1.h_hbm = bf16[8,512,1536]{2,1,0:T(8,128)(2,1)} custom-call(s32[4096]{0:T(1024)} %bitcast.7, bf16[2048,2560]{1,0:T(8,128)(2,1)} %get-tuple-element.13.xn_ref, bf16[8,2560,1536]{2,1,0:T(8,128)(2,1)} %wg_ref.1, bf16[8,2560,1536]{2,1,0:T(8,128)(2,1)} %wu_ref.1), custom_call_target="tpu_custom_call" | custom-call | flops 64424509440 | bytes 125829120 | tf_op jit(solution)/shard_map/gate_up/pallas_call | solution.py:306
  150.0 113.0 %down_reduce.1 = f32[256,2560]{1,0:T(8,128)} custom-call(s32[16384]{0:T(1024)} %bitcast.5, bf16[8,512,1536]{2,1,0:T(8,128)(2,1)} %gate_up.1.h_hbm, bf16[8,1536,2560]{2,1,0:T(8,128)(2,1)} %wd_hbm.1, f32[8,512,128]{2,1,0:T(8,128)} %get-tuple-element.14.gate_ref), custom_call_target="tpu_custom_call" | custom-call | flops 32212254720 | bytes 62914560 | tf_op jit(solution)/shard_map/down_reduce/pallas_call | solution.py:512
  263.0 3.9 %add_convert_fusion = bf16[256,2560]{1,0:T(8,128)(2,1)} fusion(f32[256,2560]{1,0:T(8,128)} %get-tuple-element.10, f32[256,2560]{1,0:T(8,128)} %down_reduce.1), kind=kLoop, calls=%fused_computation | loop fusion | flops 1310720 | bytes 6553600 | tf_op jit(solution)/shard_map/convert_element_type | solution.py:558

commit v3 on v2

--- a/solution.py
+++ b/solution.py
@@ -24,9 +24,9 @@
 
 
 def gather_kernel(x_ref, gain_ref, rw_ref, ids_ref, wsg_hbm, wsu_hbm, wsd_hbm,
-                  xn_all, base_ref, tok_ref, slot_ref, gcol_ref,
-                  xn, wsg, wsu, wsd, hid, ids_all, gates_all, cnt, gtok, cnt3, gtok3,
-                  w_sem, own_sem, meta_send, meta_recv, snd, rcv):
+                  xn_all, base_hbm, tok_ref, slot_ref, gcol_hbm,
+                  base_ref, gcol_ref, xn, wsg, wsu, wsd, hid, ids_all, gates_all, cnt, gtok, cnt3, gtok3,
+                  w_sem, own_sem, out_sem, meta_send, meta_recv, snd, rcv):
     tok_dev, d = x_ref.shape
     n_dev, top_pad = ids_all.shape[0], ids_all.shape[1]
     n_exp, tokens = cnt.shape
@@ -56,12 +56,12 @@
         d_copy(c).start()
 
     def norm(b, _):
-        at = pl.ds(pl.multiple_of(b * 16, 16), 16)
+        at = pl.ds(pl.multiple_of(b * 32, 32), 32)
         x = x_ref[at, :].astype(jnp.float32)
         inv = lax.rsqrt(jnp.mean(x * x, axis=1, keepdims=True) + NORM_EPS)
         xn[at, :] = (x * inv * gain_ref[...]).astype(jnp.bfloat16)
         return 0
-    lax.fori_loop(0, tok_dev // 16, norm, 0)
+    lax.fori_loop(0, tok_dev // 32, norm, 0)
 
     pl.semaphore_wait(barrier, n_dev - 1)
 
@@ -124,6 +124,8 @@
         base_ref[:, at] = x_ref[:, at].astype(jnp.float32) + y.astype(jnp.float32)
         return 0
     lax.fori_loop(0, nd, shared_down, 0)
+    base_out = pltpu.make_async_copy(base_ref, base_hbm, out_sem.at[0])
+    base_out.start()
 
     mine(0, 0, xdev).wait_recv()
     relay = [pass_on(6, xdev, 0, ydev)]
@@ -201,6 +203,8 @@
             tok_ref[e, :, r0:r0 + LANES] = jnp.minimum(row, float(tokens - 1)).astype(jnp.int32) * (d // LANES)
         return 0
     lax.fori_loop(0, n_exp, table, 0)
+    gcol_out = pltpu.make_async_copy(gcol_ref, gcol_hbm, out_sem.at[1])
+    gcol_out.start()
 
     pass_on(6, diag, 0, ydev).wait_recv()
     last = [pass_on(12, diag, 0, partner)]
@@ -210,6 +214,8 @@
     last[1].start()
 
     own.wait()
+    base_out.wait()
+    gcol_out.wait()
     for cp in direct + relay + side + more + last:
         cp.wait_send()
     for which in range(2):
@@ -236,8 +242,10 @@
             jax.ShapeDtypeStruct((n_exp, cap, LANES), f32),
         ),
         in_specs=[vmem, vmem, vmem, vmem, hbm, hbm, hbm],
-        out_specs=(hbm, vmem, vmem, vmem, vmem),
+        out_specs=(hbm, hbm, vmem, vmem, hbm),
         scratch_shapes=[
+            pltpu.VMEM((tok_dev, d), f32),
+            pltpu.VMEM((n_exp, cap, LANES), f32),
             pltpu.VMEM((tok_dev, d), bf16),
             pltpu.VMEM((inter // cg, d, cg), bf16),
             pltpu.VMEM((inter // cg, d, cg), bf16),
@@ -251,6 +259,7 @@
             pltpu.VMEM((n_exp, 1, tokens), f32),
             pltpu.SemaphoreType.DMA((3, max(inter // cg, d // cd))),
             pltpu.SemaphoreType.DMA,
+            pltpu.SemaphoreType.DMA((2,)),
             pltpu.SemaphoreType.DMA((2, n_dev)),
             pltpu.SemaphoreType.DMA((2, n_dev)),
             pltpu.SemaphoreType.DMA((14,)),
@@ -262,11 +271,22 @@
     )(x, gain, router_w, ids_t, ws_gate, ws_up, ws_down)
 
 
-def gate_up_kernel(tok_ref, xn_ref, wg_ref, wu_ref, h_ref, xf, gbuf, lhs):
+def gate_up_kernel(tok_ref, xn_ref, wg_ref, wu_ref, h_ref, xf, gbuf, lhs_a, lhs_b):
     e = pl.program_id(0)
     j = pl.program_id(1)
-    cap, d = lhs.shape
+    n_exp = pl.num_programs(0)
+    cap, d = lhs_a.shape
     nc = d // LANES
+    piece = gbuf.shape[0] // nc
+
+    def gather(ex, r0):
+        at = ex * cap + r0
+        for u in range(piece):
+            gbuf[pl.ds(u * nc, nc), :] = xf[pl.ds(tok_ref[at + u], nc), :]
+
+    def narrow(dst, r0):
+        for c in range(nc):
+            dst[pl.ds(r0, piece), c * LANES:(c + 1) * LANES] = gbuf[pl.ds(c, piece, stride=nc), :].astype(jnp.bfloat16)
 
     @pl.when((e == 0) & (j == 0))
     def _():
@@ -278,31 +298,36 @@
             return 0
         lax.fori_loop(0, xn_ref.shape[0] // 64, widen, 0)
 
-    @pl.when(j == 0)
+        def first(i, _):
+            r0 = pl.multiple_of(jnp.minimum(i * piece, cap - piece), 16)
+            gather(0, r0)
+            narrow(lhs_a, r0)
+            return 0
+        lax.fori_loop(0, pl.cdiv(cap, piece), first, 0)
+
+    def step(cur, nxt):
+        r0 = pl.multiple_of(jnp.minimum(j * piece, cap - piece), 16)
+        gather(jnp.minimum(e + 1, n_exp - 1), r0)
+        g = jnp.dot(cur[...], wg_ref[0], preferred_element_type=jnp.float32)
+        narrow(nxt, r0)
+        u = jnp.dot(cur[...], wu_ref[0], preferred_element_type=jnp.float32)
+        h_ref[0] = (g * jax.nn.sigmoid(g) * u).astype(jnp.bfloat16)
+
+    @pl.when(lax.rem(e, 2) == 0)
     def _():
-        def gather(b, _):
-            for u in range(16):
-                r = b * 16 + u
-                gbuf[pl.ds(r * nc, nc), :] = xf[pl.ds(tok_ref[e * cap + r], nc), :]
-            return 0
-        lax.fori_loop(0, cap // 16, gather, 0)
-
-        def narrow(b, _):
-            rows = pl.multiple_of(b * 64, 64)
-            for c in range(nc):
-                lhs[pl.ds(rows, 64), c * LANES:(c + 1) * LANES] = gbuf[pl.ds(rows * nc + c, 64, stride=nc), :].astype(jnp.bfloat16)
-            return 0
-        lax.fori_loop(0, cap // 64, narrow, 0)
-
-    g = jnp.dot(lhs[...], wg_ref[0], preferred_element_type=jnp.float32)
-    u = jnp.dot(lhs[...], wu_ref[0], preferred_element_type=jnp.float32)
-    h_ref[0] = (g * jax.nn.sigmoid(g) * u).astype(jnp.bfloat16)
+        step(lhs_a, lhs_b)
+
+    @pl.when(lax.rem(e, 2) == 1)
+    def _():
+        step(lhs_b, lhs_a)
 
 
 def gate_up(tok_off, xn_all, w_gate, w_up, block=512):
     n_exp, d, inter = w_gate.shape
     cap = tok_off.shape[0] // n_exp
     tokens = xn_all.shape[0]
+    steps = inter // block
+    piece = -(-cap // (16 * steps)) * 16
     return pl.pallas_call(
         gate_up_kernel,
         grid_spec=pltpu.PrefetchScalarGridSpec(
@@ -316,7 +341,8 @@
             out_specs=pl.BlockSpec((1, cap, block), lambda e, j, t: (e, 0, j)),
             scratch_shapes=[
                 pltpu.VMEM((tokens * d // LANES, LANES), jnp.float32),
-                pltpu.VMEM((cap * d // LANES, LANES), jnp.float32),
+                pltpu.VMEM((piece * d // LANES, LANES), jnp.float32),
+                pltpu.VMEM((cap, d), jnp.bfloat16),
                 pltpu.VMEM((cap, d), jnp.bfloat16),
             ],
         ),
@@ -460,9 +486,11 @@
             def one(b, _):
                 at = dev * (8 * tok_dev) + b * 8
                 for u in range(8):
-                    acc = ybuf[pl.ds(slot_ref[at + u], sub), :]
-                    for k in range(1, TOP):
-                        acc = acc + ybuf[pl.ds(slot_ref[at + (k * tok_dev + u)], sub), :]
+                    acc = None
+                    for k in range(TOP):
+                        table = slot_ref.at[pl.ds(k * tok_dev + u, slot_ref.shape[0] - TOP * tok_dev)]
+                        row = ybuf[pl.ds(table[at], sub), :]
+                        acc = row if acc is None else acc + row
                     part[dev, pl.ds(b * (8 * sub) + u * sub, sub), :] = acc
                 return 0
             lax.fori_loop(0, tok_dev // 8, one, 0)

time: 267 us -> 259 us (0.970)
  Pallas kernels: 259 us -> 251 us
    pallas_call x1, Pallas kernels: 89.2 us -> 83.9 us  [gate_up(): pl.pallas_call(gate_up_kernel, grid_spec=pltpu.PrefetchScalarGridSpec(num...]
where the time goes in v3:
time: 259 us
  Pallas kernels  251 us (97%)
  local copies, waits for them, and re-layouts  4.11 us (2%)
  other arithmetic  3.88 us (1%)
    pallas_call x1, Pallas kernels, down_reduce(): pl.pallas_call(down_kernel, out_shape=jax.ShapeDtypeStruct((tok_dev, d),...  112 us
    pallas_call x1, Pallas kernels, gate_up(): pl.pallas_call(gate_up_kernel, grid_spec=pltpu.PrefetchScalarGridSpec(num...  83.9 us
    pallas_call x1, Pallas kernels, gather_rows(): pl.pallas_call(gather_kernel, out_shape=(jax.ShapeDtypeStruct((tokens, d)...  54.9 us

profile of v3, /device:TPU:0, one launch (start us, length us, event | category | flops | bytes accessed | tf_op | source)
XLA Modules:
  0.0 258.6 jit_solution(15067566255714604512)
XLA Ops:
  0.0 1.3 pad.4.ids_ref
  1.3 1.3 broadcast_in_dim.3.gain_ref
  2.6 54.9 %gather_rows.1 = (bf16[2048,2560]{1,0:T(8,128)(2,1)}, f32[256,2560]{1,0:T(8,128)}, s32[8,1,512]{2,1,0:T(1,128)}, s32[64,256]{1,0:T(8,128)}, f32[8,512,128]{2,1,0:T(8,128)}) custom-call(bf16[256,2560]{1,0:T(8,128)(2,1)} %x_ref.1, f32[1,2560]{1,0:T(1,128)} %broadcast_in_dim.3.gain_ref, f32[64,2560]{1,0:T(8,128)} %rw_ref.1, s32[8,256]{1,0:T(8,128)} %pad.4.ids_ref, ...), custom_call_target="tpu_custom_call" | custom-call | flops 12079595520 | bytes 47185920 | tf_op jit(solution)/shard_map/gather_rows/pallas_call | solution.py:235
  57.5 1.5 copy.11
  59.0 83.9 %gate_up.1.h_hbm = bf16[8,512,1536]{2,1,0:T(8,128)(2,1)} custom-call(s32[4096]{0:T(1024)} %bitcast.7, bf16[2048,2560]{1,0:T(8,128)(2,1)} %get-tuple-element.13.xn_ref, bf16[8,2560,1536]{2,1,0:T(8,128)(2,1)} %wg_ref.1, bf16[8,2560,1536]{2,1,0:T(8,128)(2,1)} %wu_ref.1), custom_call_target="tpu_custom_call" | custom-call | flops 64424509440 | bytes 125829120 | tf_op jit(solution)/shard_map/gate_up/pallas_call | solution.py:331
  143.0 111.7 %down_reduce.1 = f32[256,2560]{1,0:T(8,128)} custom-call(s32[16384]{0:T(1024)} %bitcast.5, bf16[8,512,1536]{2,1,0:T(8,128)(2,1)} %gate_up.1.h_hbm, bf16[8,1536,2560]{2,1,0:T(8,128)(2,1)} %wd_hbm.1, f32[8,512,128]{2,1,0:T(8,128)} %get-tuple-element.14.gate_ref), custom_call_target="tpu_custom_call" | custom-call | flops 32212254720 | bytes 62914560 | tf_op jit(solution)/shard_map/down_reduce/pallas_call | solution.py:540
  254.7 3.9 %add_convert_fusion = bf16[256,2560]{1,0:T(8,128)(2,1)} fusion(f32[256,2560]{1,0:T(8,128)} %get-tuple-element.10, f32[256,2560]{1,0:T(8,128)} %down_reduce.1), kind=kLoop, calls=%fused_computation | loop fusion | flops 1310720 | bytes 6553600 | tf_op jit(solution)/shard_map/convert_element_type | solution.py:586
